TPU v7x, 32 devices: a whole 2x2x4 slice. The times are simulated.
32 devices in a mesh: row: 4 (over y, x), col: 8 (over z, core).
Axes of the slice: x: 2, y: 2, z: 4, core: 2. Of those that a mesh axis runs over, the one named last changes fastest.
Arguments:
- view_one: bfloat16 [2048, 8192], P('row', 'col'), may hold values from -6 to 6
- view_two: bfloat16 [2048, 8192], P('row', 'col'), may hold values from -6 to 6
- pair_weights: bfloat16 [8192, 8192], P('row', 'col'), may hold values from 0.25 to 2.5
Outputs:
- first_grad: bfloat16 [2048, 8192], P('row', 'col')
- second_grad: bfloat16 [2048, 8192], P('row', 'col')
All inputs are finite; a program needn't handle non-finite values.
Results may differ from a plain program's by a relative error of at most 0.004.
Values may be sent and summed in bfloat16 or wider, within the bound.
A program may use at most 128 MiB of HBM per device.

v0:
```python
import jax
import jax.numpy as jnp
from jax import lax
from jax.sharding import PartitionSpec as P


def per_device(view_one, view_two, pair_weights):
    wide_two = lax.all_gather(view_two, "col", axis=1, tiled=True)
    samples = view_one.shape[0] * lax.axis_size("row")
    local_rows = pair_weights.shape[0]
    local_cols = pair_weights.shape[1]
    regrouped = lax.all_to_all(wide_two, "row", split_axis=1, concat_axis=0, tiled=True)
    summed = lax.dot_general(
        regrouped,
        lax.all_gather(view_one, "row", axis=0, tiled=True),
        (((0,), (0,)), ((), ())),
        preferred_element_type=jnp.float32,
    )
    correlation = summed / samples
    row_ids = lax.axis_index("row") * local_rows + lax.broadcasted_iota(
        jnp.int32, (local_rows, local_cols), 0
    )
    col_ids = lax.axis_index("col") * local_cols + lax.broadcasted_iota(
        jnp.int32, (local_rows, local_cols), 1
    )
    identity = jnp.where(row_ids == col_ids, 1.0, 0.0).astype(jnp.float32)
    weighted = (pair_weights.astype(jnp.float32) * (correlation - identity)).astype(jnp.bfloat16)
    grad_cols = lax.all_gather(weighted, "row", axis=0, tiled=True)
    first_grad = jnp.dot(wide_two, grad_cols, preferred_element_type=jnp.float32).astype(
        jnp.bfloat16
    )
    second_flipped = lax.psum_scatter(
        lax.dot_general(
            grad_cols, view_one, (((1,), (1,)), ((), ())), preferred_element_type=jnp.float32
        ),
        "col",
        scatter_dimension=0,
        tiled=True,
    )
    return (first_grad, second_flipped.T.astype(jnp.bfloat16))


def solution(mesh):
    placed = (P("row", "col"), P("row", "col"), P("row", "col"))
    return jax.shard_map(
        per_device,
        mesh=mesh,
        in_specs=placed,
        out_specs=(P("row", "col"), P("row", "col")),
        check_vma=False,
    )
```

profile of v0, /device:TPU:0, one launch (start us, length us, event | category | flops | bytes accessed | tf_op | source)
XLA Modules:
  0.0 604.9 jit_solution(17463055193101031785)
XLA Ops:
  8.0 0.0 all-gather.4.cloned.1.call-start
  8.0 2.3 copy.9
  10.3 0.0 all-gather.4.cloned.1.call-update
  10.3 85.4 %all-gather.4.cloned.1.call-done = bf16[512,8192]{0,1:T(8,128)(2,1)} async-done(((bf16[512,1024]{0,1:T(8,128)(2,1)}), bf16[512,8192]{0,1:T(8,128)(2,1)}) %all-gather.4.cloned.1.call-update) | async-done | bytes 8388624 | tf_op jit(solution)/shard_map/all_gather | solution.py:8
  95.8 5.7 all-to-all-start
  101.4 0.0 all-gather.6.cloned.1.call-start
  101.5 0.5 all-gather.6.cloned.1.call-update
  102.0 0.0 all-gather.8.cloned.1.call-start
  102.1 126.1 %all-to-all-done = bf16[512,4,2048]{0,2,1:T(8,128)(2,1)} async-done(((bf16[512,4,2048]{0,2,1:T(8,128)(2,1)}), bf16[512,4,2048]{0,2,1:T(8,128)(2,1)}, u32[]{:S(2)}, u32[]{:S(2)}) %all-to-all-start) | async-done | bytes 8388640 | tf_op jit(solution)/shard_map/all_to_all | solution.py:12
  228.2 11.4 %copy.10 = bf16[4,512,2048]{2,1,0:T(8,128)(2,1)} copy(bf16[4,512,2048]{1,2,0:T(8,128)(2,1)} %bitcast.1) | data formatting | bytes 16777216 | tf_op jit(solution)/shard_map/all_to_all | solution.py:12
  239.6 0.0 all-gather.6.cloned.1.call-done
  239.6 0.0 copy-start
  239.6 15.8 %multiply_convert_fusion = bf16[2048,1024]{1,0:T(8,128)(2,1)} fusion(bf16[2048,1024]{1,0:T(8,128)(2,1)} %param.5, bf16[2048,2048]{1,0:T(8,128)(2,1)} %bitcast.14, bf16[2048,1024]{1,0:T(8,128)(2,1)} %all-gather.6.cloned.1.call-done, s32[1024]{0:T(1024)S(1)} %iota_add_fusion.1, s32[2048]{0:T(1024)S(1)} %iota_add_fusion), kind=kOutput, calls=%fused_computation | convolution fusion | flops 8604614656 | bytes 20983808 | tf_op jit(solution)/shard_map/dot_general | solution.py:13
  255.4 0.0 all-gather.8.cloned.1.call-update
  255.4 0.2 reduce-scatter.2.cloned.1.call-start
  255.7 154.6 %all-gather.8.cloned.1.call-done = bf16[8192,1024]{1,0:T(8,128)(2,1)} async-done(((bf16[2048,1024]{1,0:T(8,128)(2,1)}), bf16[8192,1024]{1,0:T(8,128)(2,1)}) %all-gather.8.cloned.1.call-update) | async-done | bytes 16777232 | tf_op jit(solution)/shard_map/all_gather | solution.py:28
  410.3 0.0 copy-done
  410.3 15.8 %fusion.1 = f32[8192,512]{1,0:T(8,128)} fusion(bf16[8192,1024]{1,0:T(8,128)(2,1)} %all-gather.8.cloned.1.call-done, bf16[512,1024]{1,0:T(8,128)(2,1)S(1)} %copy-done), kind=kOutput, calls=%fused_computation.6 | convolution fusion | flops 8589934592 | bytes 34603008 | tf_op jit(solution)/shard_map/dot_general | solution.py:33
  426.0 0.0 reduce-scatter.2.cloned.1.call-update
  426.1 14.8 %fusion = bf16[512,1024]{0,1:T(8,128)(2,1)S(1)} fusion(bf16[8192,1024]{1,0:T(8,128)(2,1)} %all-gather.8.cloned.1.call-done, bf16[512,8192]{0,1:T(8,128)(2,1)} %all-gather.4.cloned.1.call-done), kind=kOutput, calls=%fused_computation.2 | convolution fusion | flops 8590458880 | bytes 26214400 | tf_op jit(solution)/shard_map/dot_general | solution.py:29
  440.9 1.3 copy.11
  442.2 152.2 %reduce-scatter.2.cloned.1.call-done = f32[1024,512]{1,0:T(8,128)} async-done(((f32[8192,512]{1,0:T(8,128)}), f32[1024,512]{1,0:T(8,128)}) %reduce-scatter.2.cloned.1.call-update) | async-done | bytes 2097168 | tf_op jit(solution)/shard_map/reduce_scatter | solution.py:32
  594.4 1.7 convert_bitcast_fusion
  596.1 1.3 copy.12
  (2 shorter events, 0.0 us)
Async XLA Ops:
  8.0 87.8 %all-gather.4.cloned.1.call-start = ((), (), s32[]{:S(2)}) async-start(), calls=%async_computation.2 | async-start | bytes 9437184 | tf_op jit(solution)/shard_map/all_gather | solution.py:8
  95.8 132.4 %all-to-all-start = ((bf16[512,4,2048]{0,2,1:T(8,128)(2,1)}), bf16[512,4,2048]{0,2,1:T(8,128)(2,1)}, u32[]{:S(2)}, u32[]{:S(2)}) async-start(bf16[512,4,2048]{0,2,1:T(8,128)(2,1)} %bitcast.13), calls=%async_computation | async-start | bytes 16777216 | tf_op jit(solution)/shard_map/all_to_all | solution.py:12
  101.4 138.2 %all-gather.6.cloned.1.call-start = ((), (), s32[]{:S(2)}) async-start(), calls=%async_computation.3 | async-start | bytes 5242880 | tf_op jit(solution)/shard_map/all_gather | solution.py:15
  102.0 308.3 %all-gather.8.cloned.1.call-start = ((), (), s32[]{:S(2)}) async-start(), calls=%async_computation.4 | async-start | bytes 20971520 | tf_op jit(solution)/shard_map/all_gather | solution.py:28
  239.6 170.7 %copy-start = (bf16[512,1024]{1,0:T(8,128)(2,1)S(1)}, bf16[512,1024]{1,0:T(8,128)(2,1)}, u32[]{:S(2)}) copy-start(bf16[512,1024]{1,0:T(8,128)(2,1)} %param.3) | copy-start | bytes 3145732
  255.4 339.0 %reduce-scatter.2.cloned.1.call-start = ((), (), s32[]{:S(2)}) async-start(), calls=%async_computation.5 | async-start | bytes 18874368 | tf_op jit(solution)/shard_map/reduce_scatter | solution.py:32
Sparse Core Ops, SparseCore 0:
  11.0 84.7 all-gather.3
  426.2 168.1 reduce-scatter.1
Sparse Core Ops, SparseCore 1:
  103.8 118.6 all-gather.5
  255.5 154.7 all-gather.7
where the time goes:
time: 605 us
  waiting for transfers between devices  519 us (86%)
  matrix products  46.4 us (8%)
  local copies, waits for them, and re-layouts  16.3 us (3%)
  between operations  15.5 us (3%)
    all_gather x1, waiting for transfers between devices, per_device(): grad_cols = lax.all_gather(weighted, 'row', axis=0, tiled=True)  155 us
    reduce_scatter x1, waiting for transfers between devices, per_device(): lax.psum_scatter(lax.dot_general(grad_cols, view_one, (((1,), (1,)), ((),...  152 us
    all_to_all x1, waiting for transfers between devices, per_device(): lax.all_to_all(wide_two, 'row', split_axis=1, concat_axis=0, tiled=True)  126 us
    all_gather x1, waiting for transfers between devices, per_device(): wide_two = lax.all_gather(view_two, 'col', axis=1, tiled=True)  85.4 us
    dot_general x1, matrix products, per_device(): lax.dot_general(regrouped, lax.all_gather(view_one, 'row', axis=0, tiled=...  15.8 us
    dot_general x1, matrix products, per_device(): lax.dot_general(grad_cols, view_one, (((1,), (1,)), ((), ())), preferred_...  15.8 us
    dot_general x1, matrix products, per_device(): jnp.dot(wide_two, grad_cols, preferred_element_type=jnp.float32)  14.8 us
  transfers between devices with their start and end apart: 5, of which 4 were waited for; matrix products, arithmetic and copies ran while one was open for 5% of the time, Pallas kernels for 0%

commit v1 on v0

--- a/solution.py
+++ b/solution.py
@@ -2,6 +2,19 @@
 import jax.numpy as jnp
 from jax import lax
 from jax.sharding import PartitionSpec as P
+
+
+def answer_the_columns(unit, mesh_dim):
+    how_many = lax.axis_size(mesh_dim)
+    e_now = sorted(((src_i, (src_i + 1) % how_many) for src_i in range(how_many)))
+    v_next = unit
+    cards = [v_next]
+    for i in range(1, how_many):
+        v_next = lax.ppermute(v_next, axis_name=mesh_dim, perm=e_now)
+        cards.insert(0, v_next)
+    back = jnp.concatenate(cards, axis=0)
+    d_next = lax.axis_index(mesh_dim) + 1
+    return jnp.roll(back, d_next * unit.shape[0], axis=0)
 
 
 def per_device(view_one, view_two, pair_weights):
@@ -25,7 +38,7 @@
     )
     identity = jnp.where(row_ids == col_ids, 1.0, 0.0).astype(jnp.float32)
     weighted = (pair_weights.astype(jnp.float32) * (correlation - identity)).astype(jnp.bfloat16)
-    grad_cols = lax.all_gather(weighted, "row", axis=0, tiled=True)
+    grad_cols = answer_the_columns(weighted, "row")
     first_grad = jnp.dot(wide_two, grad_cols, preferred_element_type=jnp.float32).astype(
         jnp.bfloat16
     )

time: 605 us -> 755 us (1.25)
  waiting for transfers between devices: 519 us -> 635 us
  local copies, waits for them, and re-layouts: 16.3 us -> 48.4 us
    ppermute x0 -> x3, waiting for transfers between devices: none -> 274 us  [answer_the_columns(): v_next = lax.ppermute(v_next, axis_name=mesh_dim, perm=e_now)]
    all_gather x1 -> x0, waiting for transfers between devices: 155 us -> none  [per_device(): grad_cols = lax.all_gather(weighted, 'row', axis=0, tiled=True)]
    unnamed x5 -> x20, local copies, waits for them, and re-layouts: 4.91 us -> 34.6 us
  transfers between devices with their start and end apart: 5 -> 7, of which waited for: 4 -> 6; matrix products, arithmetic and copies ran while one was open for 5% -> 4% of each run, Pallas kernels for 0% -> 0%
where the time goes in v1:
time: 755 us; the launch traced here: 754 us
  waiting for transfers between devices  635 us (84%)
  local copies, waits for them, and re-layouts  48.4 us (6%)
  matrix products  45.8 us (6%)
  between operations  15.6 us (2%)
  starting transfers between devices  7.69 us (1%)
    ppermute x3, waiting for transfers between devices, answer_the_columns(): v_next = lax.ppermute(v_next, axis_name=mesh_dim, perm=e_now)  274 us
    reduce_scatter x1, waiting for transfers between devices, per_device(): lax.psum_scatter(lax.dot_general(grad_cols, view_one, (((1,), (1,)), ((),...  149 us
    all_to_all x1, waiting for transfers between devices, per_device(): lax.all_to_all(wide_two, 'row', split_axis=1, concat_axis=0, tiled=True)  126 us
    all_gather x1, waiting for transfers between devices, per_device(): wide_two = lax.all_gather(view_two, 'col', axis=1, tiled=True)  85.4 us
    unnamed x20, local copies, waits for them, and re-layouts  34.6 us
    dot_general x1, matrix products, per_device(): lax.dot_general(grad_cols, view_one, (((1,), (1,)), ((), ())), preferred_...  15.8 us
    dot_general x1, matrix products, per_device(): jnp.dot(wide_two, grad_cols, preferred_element_type=jnp.float32)  15.6 us
  transfers between devices with their start and end apart: 7, of which 6 were waited for; matrix products, arithmetic and copies ran while one was open for 4% of the time, Pallas kernels for 0%

profile of v1, /device:TPU:0, one launch (start us, length us, event | category | flops | bytes accessed | tf_op | source)
XLA Modules:
  0.0 754.3 jit_solution(15340180576514604440)
XLA Ops:
  8.0 0.0 all-gather.3.cloned.1.call-start
  8.0 2.3 copy.9
  10.3 0.0 all-gather.3.cloned.1.call-update
  10.3 85.4 %all-gather.3.cloned.1.call-done = bf16[512,8192]{0,1:T(8,128)(2,1)} async-done(((bf16[512,1024]{0,1:T(8,128)(2,1)}), bf16[512,8192]{0,1:T(8,128)(2,1)}) %all-gather.3.cloned.1.call-update) | async-done | bytes 8388624 | tf_op jit(solution)/shard_map/all_gather | solution.py:21
  95.8 5.6 all-to-all-start
  101.4 0.0 all-gather.5.cloned.1.call-start
  101.5 0.5 all-gather.5.cloned.1.call-update
  102.0 0.0 reduce-scatter.2.cloned.1.call-start
  102.1 126.1 %all-to-all-done = bf16[512,4,2048]{0,2,1:T(8,128)(2,1)} async-done(((bf16[512,4,2048]{0,2,1:T(8,128)(2,1)}), bf16[512,4,2048]{0,2,1:T(8,128)(2,1)}, u32[]{:S(2)}, u32[]{:S(2)}) %all-to-all-start) | async-done | bytes 8388640 | tf_op jit(solution)/shard_map/all_to_all | solution.py:25
  228.1 11.4 %copy.10 = bf16[4,512,2048]{2,1,0:T(8,128)(2,1)} copy(bf16[4,512,2048]{1,2,0:T(8,128)(2,1)} %bitcast.1) | data formatting | bytes 16777216 | tf_op jit(solution)/shard_map/all_to_all | solution.py:25
  239.6 0.0 all-gather.5.cloned.1.call-done
  239.6 14.4 %multiply_convert_fusion = bf16[2048,1024]{1,0:T(8,128)(2,1)S(1)} fusion(bf16[2048,1024]{1,0:T(8,128)(2,1)} %param.5, bf16[2048,2048]{1,0:T(8,128)(2,1)} %bitcast.12, bf16[2048,1024]{1,0:T(8,128)(2,1)} %all-gather.5.cloned.1.call-done, s32[1024]{0:T(1024)S(1)} %iota_add_fusion.1, s32[2048]{0:T(1024)S(1)} %iota_add_fusion), kind=kOutput, calls=%fused_computation.4 | convolution fusion | flops 8604614656 | bytes 20983808 | tf_op jit(solution)/shard_map/dot_general | solution.py:26
  254.0 0.0 copy-start
  254.0 1.9 copy-done
  255.9 1.4 collective-permute-start
  257.3 91.3 %collective-permute-done = bf16[2048,1024]{1,0:T(8,128)(2,1)S(1)} collective-permute-done((bf16[2048,1024]{1,0:T(8,128)(2,1)S(1)}, bf16[2048,1024]{1,0:T(8,128)(2,1)S(1)}, u32[]{:S(2)}, u32[]{:S(2)}) %collective-permute-start) | collective-permute-done | bytes 4194336 | tf_op jit(solution)/shard_map/ppermute | solution.py:13
  348.7 0.0 copy-start.2
  348.7 1.9 copy-done.2
  350.6 0.5 collective-permute-start.1
  351.2 91.5 %collective-permute-done.1 = bf16[2048,1024]{1,0:T(8,128)(2,1)} collective-permute-done((bf16[2048,1024]{1,0:T(8,128)(2,1)S(1)}, bf16[2048,1024]{1,0:T(8,128)(2,1)}, u32[]{:S(2)}, u32[]{:S(2)}) %collective-permute-start.1) | collective-permute-done | bytes 4194336 | tf_op jit(solution)/shard_map/ppermute | solution.py:13
  442.6 0.0 collective-permute-start.2
  442.6 0.0 copy-start.3
  442.6 91.3 %collective-permute-done.2 = bf16[2048,1024]{1,0:T(8,128)(2,1)} collective-permute-done((bf16[2048,1024]{1,0:T(8,128)(2,1)}, bf16[2048,1024]{1,0:T(8,128)(2,1)}, u32[]{:S(2)}, u32[]{:S(2)}) %collective-permute-start.2) | collective-permute-done | bytes 4194336 | tf_op jit(solution)/shard_map/ppermute | solution.py:13
  534.0 4.6 constant_dynamic-update-slice_fusion.7
  538.6 0.0 copy-start.1
  538.6 4.8 constant_dynamic-update-slice_fusion.6
  543.4 0.0 copy-done.3
  543.4 2.4 constant_dynamic-update-slice_fusion.5
  545.8 0.0 copy-done.1
  545.8 2.4 constant_dynamic-update-slice_fusion.4
  548.2 4.6 constant_dynamic-update-slice_fusion.3
  552.7 4.6 constant_dynamic-update-slice_fusion.2
  557.4 0.0 copy-start.4
  557.4 2.4 constant_dynamic-update-slice_fusion.1
  559.8 2.4 constant_dynamic-update-slice_fusion
  562.2 0.0 copy-done.4
  562.2 15.8 %fusion = f32[8192,512]{1,0:T(8,128)} fusion(bf16[512,1024]{1,0:T(8,128)(2,1)S(1)} %copy-done.4, bf16[16384,1024]{1,0:T(8,128)(2,1)} %constant_dynamic-update-slice_fusion, s32[]{:T(128)S(6)} %select_n.19), kind=kOutput, calls=%fused_computation | convolution fusion | flops 8589934592 | bytes 34603012 | tf_op jit(solution)/shard_map/dot_general | solution.py:46
  578.0 0.0 reduce-scatter.2.cloned.1.call-update
  578.0 15.6 %fusion.7 = bf16[512,1024]{0,1:T(8,128)(2,1)S(1)} fusion(bf16[512,8192]{0,1:T(8,128)(2,1)} %all-gather.3.cloned.1.call-done, bf16[16384,1024]{1,0:T(8,128)(2,1)} %constant_dynamic-update-slice_fusion, s32[]{:T(128)S(6)} %select_n.19), kind=kOutput, calls=%fused_computation.6 | convolution fusion | flops 8590458880 | bytes 26214404 | tf_op jit(solution)/shard_map/dot_general | solution.py:42
  593.6 1.3 copy.11
  594.9 148.9 %reduce-scatter.2.cloned.1.call-done = f32[1024,512]{1,0:T(8,128)} async-done(((f32[8192,512]{1,0:T(8,128)}), f32[1024,512]{1,0:T(8,128)}) %reduce-scatter.2.cloned.1.call-update) | async-done | bytes 2097168 | tf_op jit(solution)/shard_map/reduce_scatter | solution.py:45
  743.9 1.7 convert_bitcast_fusion
  745.6 1.3 copy.12
  (2 shorter events, 0.0 us)
Async XLA Ops:
  8.0 87.8 %all-gather.3.cloned.1.call-start = ((), (), s32[]{:S(2)}) async-start(), calls=%async_computation.2 | async-start | bytes 9437184 | tf_op jit(solution)/shard_map/all_gather | solution.py:21
  95.8 132.4 %all-to-all-start = ((bf16[512,4,2048]{0,2,1:T(8,128)(2,1)}), bf16[512,4,2048]{0,2,1:T(8,128)(2,1)}, u32[]{:S(2)}, u32[]{:S(2)}) async-start(bf16[512,4,2048]{0,2,1:T(8,128)(2,1)} %bitcast.11), calls=%async_computation | async-start | bytes 16777216 | tf_op jit(solution)/shard_map/all_to_all | solution.py:25
  101.4 138.2 %all-gather.5.cloned.1.call-start = ((), (), s32[]{:S(2)}) async-start(), calls=%async_computation.3 | async-start | bytes 5242880 | tf_op jit(solution)/shard_map/all_gather | solution.py:28
  102.0 641.9 %reduce-scatter.2.cloned.1.call-start = ((), (), s32[]{:S(2)}) async-start(), calls=%async_computation.4 | async-start | bytes 18874368 | tf_op jit(solution)/shard_map/reduce_scatter | solution.py:45
  254.0 1.9 copy-start
  255.9 92.8 %collective-permute-start = (bf16[2048,1024]{1,0:T(8,128)(2,1)S(1)}, bf16[2048,1024]{1,0:T(8,128)(2,1)S(1)}, u32[]{:S(2)}, u32[]{:S(2)}) collective-permute-start(bf16[2048,1024]{1,0:T(8,128)(2,1)S(1)} %multiply_convert_fusion), channel_id=1, source_target_pairs={{0,8},{8,16},{16,24},{24,0},{1,9},{9,17},{17,25},{25,1},{2,10},{10... | collective-permute-start | bytes 12582920 | tf_op jit(solution)/shard_map/ppermute | solution.py:13
  348.7 1.9 copy-start.2
  350.6 92.0 %collective-permute-start.1 = (bf16[2048,1024]{1,0:T(8,128)(2,1)S(1)}, bf16[2048,1024]{1,0:T(8,128)(2,1)}, u32[]{:S(2)}, u32[]{:S(2)}) collective-permute-start(bf16[2048,1024]{1,0:T(8,128)(2,1)S(1)} %collective-permute-done), channel_id=1, source_target_pairs={{0,8},{8,16},{16,24},{24,0},{1,9},{9,17},{17,25},{25,1},{2,10},{10... | collective-permute-start | bytes 12582920 | tf_op jit(solution)/shard_map/ppermute | solution.py:13
  442.6 91.4 %collective-permute-start.2 = (bf16[2048,1024]{1,0:T(8,128)(2,1)}, bf16[2048,1024]{1,0:T(8,128)(2,1)}, u32[]{:S(2)}, u32[]{:S(2)}) collective-permute-start(bf16[2048,1024]{1,0:T(8,128)(2,1)} %collective-permute-done.1), channel_id=1, source_target_pairs={{0,8},{8,16},{16,24},{24,0},{1,9},{9,17},{17,25},{25,1},{2,10},{10... | collective-permute-start | bytes 12582920 | tf_op jit(solution)/shard_map/ppermute | solution.py:13
  442.6 100.7 %copy-start.3 = (bf16[2048,1024]{1,0:T(8,128)(2,1)S(1)}, bf16[2048,1024]{1,0:T(8,128)(2,1)}, u32[]{:S(2)}) copy-start(bf16[2048,1024]{1,0:T(8,128)(2,1)} %copy-done.2) | copy-start | bytes 12582916
  538.6 7.2 copy-start.1
  557.4 4.8 copy-start.4
Sparse Core Ops, SparseCore 0:
  11.0 84.7 all-gather.2
  578.1 165.7 reduce-scatter.1
Sparse Core Ops, SparseCore 1:
  103.7 118.6 all-gather.4
